TPU v7x, 32 devices: a whole 2x2x4 slice. The times are simulated.
32 devices in a mesh: gx: 8 (over y, x, core), gy: 4 (over z).
Axes of the slice: x: 2, y: 2, z: 4, core: 2. Of those that a mesh axis runs over, the one named last changes fastest.
Arguments:
- layer_early: bfloat16 [1024, 8192], P(None, ('gx', 'gy')), may hold values from -48 to 48
- layer_late: bfloat16 [1024, 8192], P(('gx', 'gy')), may hold values from -48 to 48
Outputs:
- similarity: float32 [], replicated
- token_share: float32 [1024], P(('gx', 'gy'))
- early_rows: bfloat16 [1024, 8192], P(('gx', 'gy'))
- late_rows: bfloat16 [1024, 8192], P(('gx', 'gy'))
All inputs are finite; a program needn't handle non-finite values.
Results may differ from a plain program's by a relative error of at most 0.0015.
Values may be sent and summed in bfloat16 or wider, within the bound.
A program may use at most 128 MiB of HBM per device.

v0:
```python
import jax
import jax.numpy as jnp
from jax import lax
from jax.sharding import PartitionSpec as P


def pair_terms(left_early, left_late, right_early, right_late):
    dims = (((1,), (1,)), ((), ()))
    block_early = lax.dot_general(left_early, right_early, dims, preferred_element_type=jnp.float32)
    block_late = lax.dot_general(left_late, right_late, dims, preferred_element_type=jnp.float32)
    return (
        jnp.sum(block_early * block_late, axis=1),
        jnp.sum(block_early * block_early),
        jnp.sum(block_late * block_late),
    )


def body(layer_early, layer_late):
    total_rows = layer_early.shape[0]
    early_values = layer_early.astype(jnp.float32)
    early_cols = (early_values - jnp.mean(early_values, axis=0)).astype(jnp.bfloat16)
    late_values = layer_late.astype(jnp.float32)
    column_sums = lax.psum(jnp.sum(late_values, axis=0), ("gx", "gy"))
    late_rows = (late_values - column_sums / total_rows).astype(jnp.bfloat16)
    early_rows = lax.all_to_all(early_cols, ("gx", "gy"), split_axis=0, concat_axis=1, tiled=True)
    block_early, block_late = (
        lax.all_gather(early_rows, "gy", axis=0, tiled=True),
        lax.all_gather(late_rows, "gy", axis=0, tiled=True),
    )
    row_part, early_part, late_part = pair_terms(
        block_early,
        block_late,
        lax.all_gather(early_rows, "gx", axis=0, tiled=True),
        lax.all_gather(late_rows, "gx", axis=0, tiled=True),
    )
    own_align = lax.psum_scatter(row_part, "gy", scatter_dimension=0, tiled=True)
    total_kl, total_kk, total_ll = lax.psum(
        (jnp.sum(row_part), early_part, late_part), ("gx", "gy")
    )
    scale_norm = jnp.sqrt(total_kk * total_ll)
    similarity = total_kl / scale_norm
    token_share = total_rows * own_align / scale_norm
    return (similarity, token_share, early_rows, late_rows)


def solution(mesh):
    in_specs = (P(None, ("gx", "gy")), P(("gx", "gy"), None))
    out_specs = (P(), P(("gx", "gy")), P(("gx", "gy"), None), P(("gx", "gy"), None))
    return jax.shard_map(body, mesh=mesh, in_specs=in_specs, out_specs=out_specs, check_vma=False)
```

profile of v0, /device:TPU:0, one launch (start us, length us, event | category | flops | bytes accessed | tf_op | source)
XLA Modules:
  0.0 298.2 jit_solution(8457581897998979989)
XLA Ops:
  7.2 0.0 copy-start
  7.2 0.0 all-gather.9.cloned.1.call-start
  7.2 1.2 convert_reduce_fusion
  8.4 42.1 %psum.28 = f32[8192]{0:T(1024)S(1)} all-reduce(f32[8192]{0:T(1024)S(1)} %convert_reduce_fusion), channel_id=1, replica_groups=mesh['gx'=8,'gy'=4] {'gx','gy'}, use_global_device_ids=true, to_apply=%region_2.0 | all-reduce | flops 8192 | bytes 65536 | tf_op jit(solution)/shard_map/psum | solution.py:23
  50.6 1.9 fusion.1
  52.5 0.0 all-gather.9.cloned.1.call-update
  52.5 0.0 all-gather.11.cloned.1.call-start
  52.5 0.7 all-gather.11.cloned.1.call-update
  53.3 0.0 all-gather.5.cloned.1.call-start
  53.3 1.2 convert_reduce_fusion.1
  54.5 1.1 fusion
  55.6 28.2 %all_to_all.19 = bf16[32,32,256]{2,1,0:T(8,128)(2,1)S(1)} all-to-all(bf16[32,32,256]{2,1,0:T(8,128)(2,1)S(1)} %bitcast.12), channel_id=1, replica_groups=mesh['gx'=8,'gy'=4] {'gx','gy'}, dimensions={0} | all-to-all | bytes 1048576 | tf_op jit(solution)/shard_map/all_to_all | solution.py:25
  83.9 0.8 copy.8
  84.7 0.0 all-gather.5.cloned.1.call-update
  84.7 0.0 all-gather.7.cloned.1.call-start
  84.8 0.5 all-gather.7.cloned.1.call-update
  85.3 0.0 copy-done
  85.3 0.6 dynamic-slice
  86.6 22.4 %all-gather.9.cloned.1.call-done = bf16[128,8192]{1,0:T(8,128)(2,1)} async-done(((bf16[32,8192]{1,0:T(8,128)(2,1)}), bf16[128,8192]{1,0:T(8,128)(2,1)}) %all-gather.9.cloned.1.call-update) | async-done | bytes 2097168 | tf_op jit(solution)/shard_map/all_gather | solution.py:28
  109.0 38.1 %all-gather.11.cloned.1.call-done = bf16[256,8192]{1,0:T(8,128)(2,1)} async-done(((bf16[32,8192]{1,0:T(8,128)(2,1)}), bf16[256,8192]{1,0:T(8,128)(2,1)}) %all-gather.11.cloned.1.call-update) | async-done | bytes 4194320 | tf_op jit(solution)/shard_map/all_gather | solution.py:34
  147.1 4.4 %fusion.3 = f32[128,256]{1,0:T(8,128)S(1)} fusion(bf16[128,8192]{1,0:T(8,128)(2,1)} %all-gather.9.cloned.1.call-done, bf16[256,8192]{1,0:T(8,128)(2,1)} %all-gather.11.cloned.1.call-done), kind=kOutput, calls=%fused_computation.14 | convolution fusion | flops 536870912 | bytes 6422528 | tf_op jit(solution)/shard_map/dot_general | solution.py:10
  151.5 43.5 %all-gather.5.cloned.1.call-done = bf16[128,8192]{1,0:T(8,128)(2,1)} async-done(((bf16[32,8192]{1,0:T(8,128)(2,1)}), bf16[128,8192]{1,0:T(8,128)(2,1)}) %all-gather.5.cloned.1.call-update) | async-done | bytes 2097168 | tf_op jit(solution)/shard_map/all_gather | solution.py:27
  195.0 37.7 %all-gather.7.cloned.1.call-done = bf16[256,8192]{1,0:T(8,128)(2,1)} async-done(((bf16[32,8192]{1,0:T(8,128)(2,1)}), bf16[256,8192]{1,0:T(8,128)(2,1)}) %all-gather.7.cloned.1.call-update) | async-done | bytes 4194320 | tf_op jit(solution)/shard_map/all_gather | solution.py:33
  232.7 5.0 %multiply_reduce_fusion.2 = (f32[128]{0:T(128)S(1)}, f32[]{:T(128)}, f32[]{:T(128)}, f32[]{:T(128)}) fusion(f32[128,256]{1,0:T(8,128)S(1)} %fusion.3, bf16[128,8192]{1,0:T(8,128)(2,1)} %all-gather.5.cloned.1.call-done, bf16[256,8192]{1,0:T(8,128)(2,1)} %all-gather.7.cloned.1.call-done), kind=kOutput, calls=%fused_computation.8 | convolution fusion | flops 537100160 | bytes 6423052 | tf_op jit(solution)/shard_map/dot_general | solution.py:9
  237.7 39.6 %all-reduce.1 = (f32[]{:T(128)}, f32[]{:T(128)}, f32[]{:T(128)}) all-reduce(f32[]{:T(128)} %get-tuple-element.5, f32[]{:T(128)} %get-tuple-element.7, f32[]{:T(128)} %get-tuple-element.6), channel_id=1, replica_groups=mesh['gx'=8,'gy'=4] {'gx','gy'}, use_global_device_ids=true, to_apply=%region_4.0 | all-reduce | flops 3 | bytes 24 | tf_op jit(solution)/shard_map/psum | solution.py:37
  278.7 10.6 %all-reduce = f32[128]{0:T(128)S(1)} all-reduce(f32[128]{0:T(128)S(1)} %get-tuple-element.4), channel_id=2, replica_groups=mesh['gx'=8,'gy'=4] {'gy'}, use_global_device_ids=true, to_apply=%region_10.0.clone | all-reduce | flops 128 | bytes 1024
  290.0 0.6 fusion.2
  (2 shorter events, 0.0 us)
Async XLA Ops:
  7.2 78.2 %copy-start = (u32[32]{0:T(128)S(1)}, u32[32]{0:T(128)}, u32[]{:S(2)}) copy-start(u32[32]{0:T(128)} %constant.11) | copy-start | bytes 388
  7.2 101.8 %all-gather.9.cloned.1.call-start = ((), (), s32[]{:S(2)}) async-start(), calls=%async_computation.3 | async-start | bytes 2621440 | tf_op jit(solution)/shard_map/all_gather | solution.py:28
  52.5 94.6 %all-gather.11.cloned.1.call-start = ((), (), s32[]{:S(2)}) async-start(), calls=%async_computation.4 | async-start | bytes 4718592 | tf_op jit(solution)/shard_map/all_gather | solution.py:34
  53.3 141.7 %all-gather.5.cloned.1.call-start = ((), (), s32[]{:S(2)}) async-start(), calls=%async_computation.1 | async-start | bytes 2621440 | tf_op jit(solution)/shard_map/all_gather | solution.py:27
  84.7 147.9 %all-gather.7.cloned.1.call-start = ((), (), s32[]{:S(2)}) async-start(), calls=%async_computation.2 | async-start | bytes 4718592 | tf_op jit(solution)/shard_map/all_gather | solution.py:33
Sparse Core Ops, SparseCore 0:
  52.6 56.3 all-gather.8
  111.5 35.5 all-gather.10
  149.3 45.6 all-gather.4
  197.3 35.3 all-gather.6
where the time goes:
time: 299 us; the launch traced here: 298 us
  waiting for transfers between devices  143 us (48%)
  blocking collectives  121 us (40%)
  between operations  17.6 us (6%)
  matrix products  9.4 us (3%)
  other arithmetic  6.03 us (2%)
    all_gather x1, waiting for transfers between devices, body(): lax.all_gather(early_rows, 'gy', axis=0, tiled=True)  43.5 us
    psum x1, blocking collectives, body(): column_sums = lax.psum(jnp.sum(late_values, axis=0), ('gx', 'gy'))  42.1 us
    psum x1, blocking collectives, body(): lax.psum((jnp.sum(row_part), early_part, late_part), ('gx', 'gy'))  39.6 us
    all_gather x1, waiting for transfers between devices, body(): lax.all_gather(late_rows, 'gx', axis=0, tiled=True)  38.1 us
    all_gather x1, waiting for transfers between devices, body(): lax.all_gather(early_rows, 'gx', axis=0, tiled=True)  37.7 us
    all_to_all x1, blocking collectives, body(): lax.all_to_all(early_cols, ('gx', 'gy'), split_axis=0, concat_axis=1, til...  28.2 us
    all_gather x1, waiting for transfers between devices, body(): lax.all_gather(late_rows, 'gy', axis=0, tiled=True)  22.4 us
    unnamed x1, blocking collectives  10.6 us
  transfers between devices with their start and end apart: 4, of which 4 were waited for; matrix products, arithmetic and copies ran while one was open for 3% of the time, Pallas kernels for 0%

commit v1 on v0

--- a/solution.py
+++ b/solution.py
@@ -20,7 +20,7 @@
     early_values = layer_early.astype(jnp.float32)
     early_cols = (early_values - jnp.mean(early_values, axis=0)).astype(jnp.bfloat16)
     late_values = layer_late.astype(jnp.float32)
-    column_sums = lax.psum(jnp.sum(late_values, axis=0), ("gx", "gy"))
+    column_sums = jnp.sum(lax.all_gather(jnp.sum(late_values, axis=0), ("gx", "gy")), axis=0)
     late_rows = (late_values - column_sums / total_rows).astype(jnp.bfloat16)
     early_rows = lax.all_to_all(early_cols, ("gx", "gy"), split_axis=0, concat_axis=1, tiled=True)
     block_early, block_late = (

time: 299 us -> 314 us (1.050)
  waiting for transfers between devices: 143 us -> 204 us
  blocking collectives: 121 us -> 75 us
    all_gather x0 -> x1, waiting for transfers between devices: none -> 59 us  [body(): lax.all_gather(jnp.sum(late_values, axis=0), ('gx', 'gy'))]
    psum x1 -> x0, blocking collectives: 42.1 us -> none  [body(): column_sums = lax.psum(jnp.sum(late_values, axis=0), ('gx', 'gy'))]
    all_to_all x1, blocking collectives: 28.2 us -> 24.8 us  [body(): lax.all_to_all(early_cols, ('gx', 'gy'), split_axis=0, concat_axis=1, til...]
  transfers between devices with their start and end apart: 4 -> 5, of which waited for: 4 -> 5; matrix products, arithmetic and copies ran while one was open for 3% -> 2% of each run, Pallas kernels for 0% -> 0%
where the time goes in v1:
time: 314 us; the launch traced here: 313 us
  waiting for transfers between devices  204 us (65%)
  blocking collectives  75 us (24%)
  between operations  17.7 us (6%)
  matrix products  9.4 us (3%)
  other arithmetic  3.69 us (1%)
    all_gather x1, waiting for transfers between devices, body(): lax.all_gather(jnp.sum(late_values, axis=0), ('gx', 'gy'))  59 us
    all_gather x1, waiting for transfers between devices, body(): lax.all_gather(early_rows, 'gy', axis=0, tiled=True)  43.3 us
    psum x1, blocking collectives, body(): lax.psum((jnp.sum(row_part), early_part, late_part), ('gx', 'gy'))  39.6 us
    all_gather x1, waiting for transfers between devices, body(): lax.all_gather(late_rows, 'gx', axis=0, tiled=True)  38.1 us
    all_gather x1, waiting for transfers between devices, body(): lax.all_gather(early_rows, 'gx', axis=0, tiled=True)  37.7 us
    all_gather x1, waiting for transfers between devices, body(): lax.all_gather(late_rows, 'gy', axis=0, tiled=True)  25.1 us
    all_to_all x1, blocking collectives, body(): lax.all_to_all(early_cols, ('gx', 'gy'), split_axis=0, concat_axis=1, til...  24.8 us
    unnamed x1, blocking collectives  10.6 us
  transfers between devices with their start and end apart: 5, of which 5 were waited for; matrix products, arithmetic and copies ran while one was open for 2% of the time, Pallas kernels for 0%

profile of v1, /device:TPU:0, one launch (start us, length us, event | category | flops | bytes accessed | tf_op | source)
XLA Modules:
  0.0 313.2 jit_solution(8967454609239562166)
XLA Ops:
  7.2 0.0 copy-start.1
  7.2 0.0 copy-start
  7.2 0.0 all-gather.15.cloned.1.call-start
  7.2 1.9 convert_reduce_fusion
  9.1 0.0 all-gather.15.cloned.1.call-update
  9.1 0.0 all-gather.11.cloned.1.call-start
  9.2 59.0 %all-gather.15.cloned.1.call-done = f32[262144]{0:T(1024)} async-done(((f32[8192]{0:T(1024)}), f32[262144]{0:T(1024)}) %all-gather.15.cloned.1.call-update) | async-done | bytes 1048592 | tf_op jit(solution)/shard_map/all_gather | solution.py:23
  68.1 1.4 reshape.17
  69.5 0.0 copy-start.2
  69.5 0.1 reduce_sum.65
  69.7 0.0 copy-done.1
  69.7 0.9 fusion.1
  70.6 0.0 all-gather.11.cloned.1.call-update
  70.6 0.0 all-gather.13.cloned.1.call-start
  70.6 0.7 all-gather.13.cloned.1.call-update
  71.3 0.0 all-gather.7.cloned.1.call-start
  71.4 0.0 copy-done
  71.4 0.2 convert_reduce_fusion.1
  71.5 0.1 fusion
  71.7 24.8 %all_to_all.19 = bf16[32,32,256]{2,1,0:T(8,128)(2,1)S(1)} all-to-all(bf16[32,32,256]{2,1,0:T(8,128)(2,1)S(1)} %bitcast.12), channel_id=1, replica_groups=mesh['gx'=8,'gy'=4] {'gx','gy'}, dimensions={0} | all-to-all | bytes 1048576 | tf_op jit(solution)/shard_map/all_to_all | solution.py:25
  96.5 0.8 copy.9
  97.3 0.0 all-gather.7.cloned.1.call-update
  97.3 0.0 all-gather.9.cloned.1.call-start
  97.4 0.5 all-gather.9.cloned.1.call-update
  97.9 0.0 copy-done.2
  97.9 0.6 dynamic-slice
  99.1 25.1 %all-gather.11.cloned.1.call-done = bf16[128,8192]{1,0:T(8,128)(2,1)} async-done(((bf16[32,8192]{1,0:T(8,128)(2,1)}), bf16[128,8192]{1,0:T(8,128)(2,1)}) %all-gather.11.cloned.1.call-update) | async-done | bytes 2097168 | tf_op jit(solution)/shard_map/all_gather | solution.py:28
  124.2 38.1 %all-gather.13.cloned.1.call-done = bf16[256,8192]{1,0:T(8,128)(2,1)} async-done(((bf16[32,8192]{1,0:T(8,128)(2,1)}), bf16[256,8192]{1,0:T(8,128)(2,1)}) %all-gather.13.cloned.1.call-update) | async-done | bytes 4194320 | tf_op jit(solution)/shard_map/all_gather | solution.py:34
  162.3 4.4 %fusion.3 = f32[128,256]{1,0:T(8,128)S(1)} fusion(bf16[128,8192]{1,0:T(8,128)(2,1)} %all-gather.11.cloned.1.call-done, bf16[256,8192]{1,0:T(8,128)(2,1)} %all-gather.13.cloned.1.call-done), kind=kOutput, calls=%fused_computation.14 | convolution fusion | flops 536870912 | bytes 6422528 | tf_op jit(solution)/shard_map/dot_general | solution.py:10
  166.7 43.3 %all-gather.7.cloned.1.call-done = bf16[128,8192]{1,0:T(8,128)(2,1)} async-done(((bf16[32,8192]{1,0:T(8,128)(2,1)}), bf16[128,8192]{1,0:T(8,128)(2,1)}) %all-gather.7.cloned.1.call-update) | async-done | bytes 2097168 | tf_op jit(solution)/shard_map/all_gather | solution.py:27
  210.0 37.7 %all-gather.9.cloned.1.call-done = bf16[256,8192]{1,0:T(8,128)(2,1)} async-done(((bf16[32,8192]{1,0:T(8,128)(2,1)}), bf16[256,8192]{1,0:T(8,128)(2,1)}) %all-gather.9.cloned.1.call-update) | async-done | bytes 4194320 | tf_op jit(solution)/shard_map/all_gather | solution.py:33
  247.7 5.0 %multiply_reduce_fusion.2 = (f32[128]{0:T(128)S(1)}, f32[]{:T(128)}, f32[]{:T(128)}, f32[]{:T(128)}) fusion(f32[128,256]{1,0:T(8,128)S(1)} %fusion.3, bf16[128,8192]{1,0:T(8,128)(2,1)} %all-gather.7.cloned.1.call-done, bf16[256,8192]{1,0:T(8,128)(2,1)} %all-gather.9.cloned.1.call-done), kind=kOutput, calls=%fused_computation.8 | convolution fusion | flops 537100160 | bytes 6423052 | tf_op jit(solution)/shard_map/dot_general | solution.py:9
  252.8 39.6 %all-reduce.1 = (f32[]{:T(128)}, f32[]{:T(128)}, f32[]{:T(128)}) all-reduce(f32[]{:T(128)} %get-tuple-element.5, f32[]{:T(128)} %get-tuple-element.7, f32[]{:T(128)} %get-tuple-element.6), channel_id=1, replica_groups=mesh['gx'=8,'gy'=4] {'gx','gy'}, use_global_device_ids=true, to_apply=%region_4.0 | all-reduce | flops 3 | bytes 24 | tf_op jit(solution)/shard_map/psum | solution.py:37
  293.7 10.6 %all-reduce = f32[128]{0:T(128)S(1)} all-reduce(f32[128]{0:T(128)S(1)} %get-tuple-element.4), channel_id=3, replica_groups=mesh['gx'=8,'gy'=4] {'gy'}, use_global_device_ids=true, to_apply=%region_10.0.clone | all-reduce | flops 128 | bytes 1024
  305.0 0.6 fusion.2
  (2 shorter events, 0.0 us)
Async XLA Ops:
  7.2 62.5 %copy-start.1 = (bf16[32,8192]{1,0:T(8,128)(2,1)S(1)}, bf16[32,8192]{1,0:T(8,128)(2,1)}, u32[]{:S(2)}) copy-start(bf16[32,8192]{1,0:T(8,128)(2,1)} %param.3) | copy-start | bytes 1572868
  7.2 64.2 %copy-start = (bf16[1024,256]{1,0:T(8,128)(2,1)S(1)}, bf16[1024,256]{1,0:T(8,128)(2,1)}, u32[]{:S(2)}) copy-start(bf16[1024,256]{1,0:T(8,128)(2,1)} %param.2) | copy-start | bytes 1572868
  7.2 60.9 %all-gather.15.cloned.1.call-start = ((), (), s32[]{:S(2)}) async-start(), calls=%async_computation.5 | async-start | bytes 1081344 | tf_op jit(solution)/shard_map/all_gather | solution.py:23
  9.1 115.1 %all-gather.11.cloned.1.call-start = ((), (), s32[]{:S(2)}) async-start(), calls=%async_computation.3 | async-start | bytes 2621440 | tf_op jit(solution)/shard_map/all_gather | solution.py:28
  69.5 28.4 %copy-start.2 = (u32[32]{0:T(128)S(1)}, u32[32]{0:T(128)}, u32[]{:S(2)}) copy-start(u32[32]{0:T(128)} %constant.11) | copy-start | bytes 388
  70.6 91.7 %all-gather.13.cloned.1.call-start = ((), (), s32[]{:S(2)}) async-start(), calls=%async_computation.4 | async-start | bytes 4718592 | tf_op jit(solution)/shard_map/all_gather | solution.py:34
  71.3 138.7 %all-gather.7.cloned.1.call-start = ((), (), s32[]{:S(2)}) async-start(), calls=%async_computation.1 | async-start | bytes 2621440 | tf_op jit(solution)/shard_map/all_gather | solution.py:27
  97.3 150.4 %all-gather.9.cloned.1.call-start = ((), (), s32[]{:S(2)}) async-start(), calls=%async_computation.2 | async-start | bytes 4718592 | tf_op jit(solution)/shard_map/all_gather | solution.py:33
Sparse Core Ops, SparseCore 0:
  11.6 56.5 all-gather.14
  70.7 53.4 all-gather.10
  126.7 35.5 all-gather.12
  164.3 45.6 all-gather.6
  212.3 35.3 all-gather.8
